TPU v7x, 32 devices: a whole 2x2x4 slice. The times are simulated.
32 devices in a mesh: dap: 8 (over z, x), cplx: 4 (over y, core).
Axes of the slice: x: 2, y: 2, z: 4, core: 2. Of those that a mesh axis runs over, the one named last changes fastest.
Arguments:
- pair: bfloat16 [96, 384, 128], P('dap', 'cplx'), parts along dimension 1, may hold values from -6 to 6
- cotangent: bfloat16 [96, 384, 128], P('dap', 'cplx'), parts along dimension 1, may hold values from -6 to 6
- residue_mask: int32 [384], P('cplx'), parts along dimension 0, may hold values 0 or 1
- chain_ids: int32 [384], P('cplx'), parts along dimension 0, may hold values from 0 to 2, never falling along the last dimension, each value on 1 to 48 neighbouring positions
- chain_embed: float32 [2, 128], replicated, may hold values from -4 to 4
- out_norm_gain: float32 [128], replicated, may hold values from 0.25 to 1.75
- out_proj: bfloat16 [128, 512], replicated, may hold values from -0.5 to 0.5
- out_gate: bfloat16 [128, 128], replicated, may hold values from -0.5 to 0.5
- out_mid_gain: float32 [128], replicated, may hold values from 0.25 to 1.75
- out_final: bfloat16 [128, 128], replicated, may hold values from -0.5 to 0.5
- in_norm_gain: float32 [128], replicated, may hold values from 0.25 to 1.75
- in_proj: bfloat16 [128, 512], replicated, may hold values from -0.5 to 0.5
- in_gate: bfloat16 [128, 128], replicated, may hold values from -0.5 to 0.5
- in_mid_gain: float32 [128], replicated, may hold values from 0.25 to 1.75
- in_final: bfloat16 [128, 128], replicated, may hold values from -0.5 to 0.5
Outputs:
- pair_grad: bfloat16 [96, 384, 128], P('dap', 'cplx'), parts along dimension 1
- grad_proj: float32 [512, 512], P('cplx'), parts along dimension 0
- grad_gate: float32 [512, 128], P('cplx'), parts along dimension 0
- grad_final: float32 [512, 128], P('cplx'), parts along dimension 0
- grad_norm_gain: float32 [512], P('cplx'), parts along dimension 0
- grad_mid_gain: float32 [512], P('cplx'), parts along dimension 0
There are 4 independent parts, one for each index of `cplx`. A program takes and returns all parts, laid end to end along the dimension named above; an argument that names none is the same for every part. Nothing has to cross between parts.
Inputs may be any that keep to these rules, and one draw needn't show every extreme that they name: `chain_ids`: chain numbers never fall along the residues; each chain has at most 48 residues.
All inputs are finite; a program needn't handle non-finite values.
Results may differ from a plain program's by a relative error of at most 0.019.
Values may be sent and summed in bfloat16 or wider, within the bound.
A program may use at most 128 MiB of HBM per device.

v0:
```python
import jax
import jax.numpy as jnp
from jax import lax
from jax.sharding import PartitionSpec as P


def layer_norm(values_in, gain):
    average = jnp.mean(values_in, axis=-1, keepdims=True)
    centred = values_in - average
    variance = jnp.mean(centred * centred, axis=-1, keepdims=True)
    return centred * lax.rsqrt(variance + 1e-05) * gain


def gated_pair(projected, pair_mask, hidden_width):
    masked = pair_mask[..., None]
    left_act = (
        masked
        * jax.nn.sigmoid(projected[..., :hidden_width])
        * projected[..., hidden_width : 2 * hidden_width]
    )
    right_act = (
        masked
        * jax.nn.sigmoid(projected[..., 2 * hidden_width : 3 * hidden_width])
        * projected[..., 3 * hidden_width :]
    )
    return (left_act, right_act)


def shards(
    pair,
    cotangent,
    residue_mask,
    chain_ids,
    chain_embed,
    out_norm_gain,
    out_proj,
    out_gate,
    out_mid_gain,
    out_final,
    in_norm_gain,
    in_proj,
    in_gate,
    in_mid_gain,
    in_final,
):
    f32 = jnp.float32
    bf16 = jnp.bfloat16
    row_count = pair.shape[0]
    res_count = pair.shape[1]
    hidden_width = out_final.shape[0]
    inv_count = 1.0 / res_count
    row_start = lax.axis_index("dap") * row_count
    row_mask = lax.dynamic_slice_in_dim(residue_mask, row_start, row_count, 0)
    row_chain = lax.dynamic_slice_in_dim(chain_ids, row_start, row_count, 0)
    pair_mask = (row_mask[:, None] * residue_mask[None, :]).astype(f32)
    same_chain = row_chain[:, None] == chain_ids[None, :]
    start = pair.astype(f32) + jnp.where(same_chain[..., None], chain_embed[1], chain_embed[0])
    out_normed = layer_norm(start, out_norm_gain).astype(bf16)
    projected = jnp.dot(out_normed, out_proj, preferred_element_type=f32)
    left_act, right_act = gated_pair(projected, pair_mask, hidden_width)
    left_b = left_act.astype(bf16)
    right_b = right_act.astype(bf16)
    x_out = jnp.einsum(
        "ikc,jkc->ijc",
        left_b,
        lax.all_gather(right_b, "dap", axis=0, tiled=True),
        preferred_element_type=f32,
    )
    y_out = layer_norm(x_out, out_mid_gain).astype(bf16)
    update = jax.nn.sigmoid(jnp.dot(out_normed, out_gate, preferred_element_type=f32)) * jnp.dot(
        y_out, out_final, preferred_element_type=f32
    )
    pair_mid = (start + update).astype(bf16)
    mid_f32 = pair_mid.astype(f32)
    normed_f32, norm_back = jax.vjp(layer_norm, mid_f32, in_norm_gain)
    in_normed = normed_f32.astype(bf16)
    proj_in = jnp.dot(in_normed, in_proj, preferred_element_type=f32)
    (left_in, right_in), glu_back = jax.vjp(
        lambda proj_val: gated_pair(proj_val, pair_mask, hidden_width), proj_in
    )
    left_ib = left_in.astype(bf16)
    right_ib = right_in.astype(bf16)
    columns = lax.all_to_all(left_ib, "dap", split_axis=1, concat_axis=0, tiled=True)
    left_block = columns
    x_in = jnp.einsum(
        "kic,kjc->ijc",
        left_block,
        lax.all_gather(right_ib, "dap", axis=0, tiled=True),
        preferred_element_type=f32,
    )
    y_f32, mid_back = jax.vjp(layer_norm, x_in, in_mid_gain)
    y_in = y_f32.astype(bf16)
    logit = jnp.dot(in_normed, in_gate, preferred_element_type=f32)
    value = jnp.dot(y_in, in_final, preferred_element_type=f32)
    sigma = jax.nn.sigmoid(logit)
    upstream = cotangent.astype(f32)
    grad_value = (upstream * sigma).astype(bf16)
    grad_logit = (upstream * value * sigma * (1.0 - sigma)).astype(bf16)
    grad_final = jnp.einsum("ijc,ijd->cd", y_in, grad_value, preferred_element_type=f32) * inv_count
    grad_gate = (
        jnp.einsum("ijc,ijd->cd", in_normed, grad_logit, preferred_element_type=f32) * inv_count
    )
    grad_y = jnp.dot(grad_value, in_final.T, preferred_element_type=f32)
    grad_x, grad_mid = mid_back(grad_y)
    grad_x_b = grad_x.astype(bf16)
    shard_rows = lax.all_gather(grad_x_b, "dap", axis=0, tiled=True)
    left_block = left_ib
    grad_right = jnp.einsum("kic,ijc->kjc", left_block, shard_rows, preferred_element_type=f32)
    new_block = jnp.einsum("kjc,ijc->kic", right_ib, shard_rows, preferred_element_type=f32)
    grad_p = glu_back((new_block, grad_right))[0].astype(bf16)
    grad_proj = jnp.einsum("ijc,ijd->cd", in_normed, grad_p, preferred_element_type=f32) * inv_count
    grad_normed = jnp.dot(grad_p, in_proj.T, preferred_element_type=f32) + jnp.dot(
        grad_logit, in_gate.T, preferred_element_type=f32
    )
    grad_z, grad_norm = norm_back(grad_normed)
    pair_grad = (upstream + grad_z).astype(bf16)
    reduced = (
        lax.psum(grad_proj.astype(jnp.bfloat16), "dap").astype(jnp.float32),
        lax.psum(grad_gate.astype(jnp.bfloat16), "dap").astype(jnp.float32),
        lax.psum(grad_final.astype(jnp.bfloat16), "dap").astype(jnp.float32),
        lax.psum((grad_norm * inv_count).astype(jnp.bfloat16), "dap").astype(jnp.float32),
        lax.psum((grad_mid * inv_count).astype(jnp.bfloat16), "dap").astype(jnp.float32),
    )
    return (pair_grad, reduced[0], reduced[1], reduced[2], reduced[3], reduced[4])


def solution(mesh):
    placed = (
        P("dap", "cplx", None),
        P("dap", "cplx", None),
        P("cplx"),
        P("cplx"),
        P(),
        P(),
        P(),
        P(),
        P(),
        P(),
        P(),
        P(),
        P(),
        P(),
        P(),
    )
    return jax.shard_map(
        shards,
        mesh=mesh,
        in_specs=placed,
        out_specs=(
            P("dap", "cplx", None),
            P("cplx", None),
            P("cplx", None),
            P("cplx", None),
            P("cplx"),
            P("cplx"),
        ),
        check_vma=False,
    )
```

profile of v0, /device:TPU:0, one launch (start us, length us, event | category | flops | bytes accessed | tf_op | source)
XLA Modules:
  0.0 371.3 jit_solution(1143531026395006253)
XLA Ops:
  10.9 1.6 multiply_reduce_fusion.7
  13.9 1.9 fusion.47
  18.3 1.7 fusion.8
  19.9 51.8 %all-gather.4.cloned.1.call-done = bf16[96,96,128]{2,1,0:T(8,128)(2,1)} async-done(((bf16[12,96,128]{2,1,0:T(8,128)(2,1)}), bf16[96,96,128]{2,1,0:T(8,128)(2,1)}) %all-gather.4.cloned.1.call-update) | async-done | bytes 2359312 | tf_op jit(solution)/shard_map/all_gather | solution.py:66
  71.7 3.5 copy.46
  75.2 2.8 fusion.62
  84.9 3.5 all-to-all-start
  89.5 17.3 %all-to-all-done = bf16[12,96,128]{2,0,1:T(8,128)(2,1)S(1)} async-done(((bf16[12,96,128]{2,0,1:T(8,128)(2,1)}), bf16[12,96,128]{2,0,1:T(8,128)(2,1)S(1)}, u32[]{:S(2)}, u32[]{:S(2)}) %all-to-all-start) | async-done | bytes 294944 | tf_op jit(solution)/shard_map/all_to_all | solution.py:83
  108.2 29.5 %all-gather.6.cloned.1.call-done = bf16[96,96,128]{2,1,0:T(8,128)(2,1)} async-done(((bf16[12,96,128]{2,1,0:T(8,128)(2,1)}), bf16[96,96,128]{2,1,0:T(8,128)(2,1)}) %all-gather.6.cloned.1.call-update) | async-done | bytes 2359312 | tf_op jit(solution)/shard_map/all_gather | solution.py:88
  137.7 3.5 copy.52
  141.3 3.0 fusion.64
  144.2 1.6 copy.54
  147.7 1.5 add_convert_fusion.1
  155.7 44.1 %all-gather.8.cloned.1.call-done = bf16[96,96,128]{2,1,0:T(8,128)(2,1)} async-done(((bf16[12,96,128]{2,1,0:T(8,128)(2,1)}), bf16[96,96,128]{2,1,0:T(8,128)(2,1)}) %all-gather.8.cloned.1.call-update) | async-done | bytes 2359312 | tf_op jit(solution)/shard_map/all_gather | solution.py:106
  199.8 3.5 copy.55
  203.3 3.8 %fusion.66 = f32[128,96,12]{1,2,0:T(8,128)} fusion(bf16[96,96,128]{1,0,2:T(8,128)(2,1)S(1)} %copy.55, bf16[12,96,128]{1,0,2:T(8,128)(2,1)} %copy.59), kind=kOutput, calls=%fused_computation.126 | convolution fusion | flops 28311552 | bytes 3244032 | tf_op jit(solution)/shard_map/kjc,ijc->kic/dot_general | solution.py:109
  207.1 2.4 copy.60
  209.4 2.9 fusion.65
  212.4 1.5 copy.57
  213.9 2.4 bitcast_multiply_fusion.3
  220.8 1.5 fusion.19
  222.3 66.6 %all-reduce.10.cloned.1.call-done = (bf16[128,128]{1,0:T(8,128)(2,1)}, bf16[128,128]{1,0:T(8,128)(2,1)}, bf16[128]{0:T(256)(128)(2,1)}, bf16[128]{0:T(256)(128)(2,1)}) async-done(((bf16[128,128]{1,0:T(8,128)(2,1)}, bf16[128,128]{1,0:T(8,128)(2,1)}, bf16[128]{0:T(256)(128)(2,1)}, bf16[128]{0:T(256)(128)(2,1)}), (bf16[128,128]{1,0:T(8,128)(2,1)}, bf16[128,128]{1,0:T(8,128)(2,1)}, bf16[128]{0:T(256)(128)(2,1)}, ...) | async-done | bytes 66064 | tf_op jit(solution)/shard_map/psum | solution.py:119
  293.9 69.3 %all-reduce.8.cloned.1.call-done = bf16[128,512]{1,0:T(8,128)(2,1)} async-done(((bf16[128,512]{1,0:T(8,128)(2,1)}), bf16[128,512]{1,0:T(8,128)(2,1)}) %all-reduce.8.cloned.1.call-update) | async-done | bytes 131088 | tf_op jit(solution)/shard_map/psum | solution.py:118
  363.2 1.6 convert_element_type.107
  (111 shorter events, 34.5 us)
Async XLA Ops:
  7.2 73.9 %copy-start = (bf16[128,512]{1,0:T(8,128)(2,1)S(1)}, bf16[128,512]{1,0:T(8,128)(2,1)}, u32[]{:S(2)}) copy-start(bf16[128,512]{1,0:T(8,128)(2,1)} %param.26) | copy-start | bytes 393220
  7.2 64.5 %all-gather.4.cloned.1.call-start = ((), (), s32[]{:S(2)}) async-start(), calls=%async_computation.1 | async-start | bytes 2654208 | tf_op jit(solution)/shard_map/all_gather | solution.py:66
  15.9 2.4 copy-start.5
  15.9 2.4 copy-start.23
  15.9 2.4 copy-start.25
  17.0 120.7 %all-gather.6.cloned.1.call-start = ((), (), s32[]{:S(2)}) async-start(), calls=%async_computation.2 | async-start | bytes 2654208 | tf_op jit(solution)/shard_map/all_gather | solution.py:88
  75.2 3.1 copy-start.24
  78.1 2.6 copy-start.22
  81.1 7.4 %copy-start.14 = (bf16[12,96,128]{2,1,0:T(8,128)(2,1)}, bf16[12,96,128]{2,1,0:T(8,128)(2,1)S(1)}, u32[]{:S(2)}) copy-start(bf16[12,96,128]{2,1,0:T(8,128)(2,1)S(1)} %multiply_convert_fusion.4) | copy-start | bytes 884740
  81.5 1.4 copy-start.1
  82.9 5.5 %copy-start.20 = (bf16[128,128]{1,0:T(8,128)(2,1)S(1)}, bf16[128,128]{1,0:T(8,128)(2,1)}, u32[]{:S(2)}) copy-start(bf16[128,128]{1,0:T(8,128)(2,1)} %param.27) | copy-start | bytes 98308
  84.0 22.9 %copy-start.9 = (bf16[12,96,128]{2,1,0:T(8,128)(2,1)}, bf16[12,96,128]{2,1,0:T(8,128)(2,1)S(1)}, u32[]{:S(2)}) copy-start(bf16[12,96,128]{2,1,0:T(8,128)(2,1)S(1)} %get-tuple-element.22) | copy-start | bytes 884740
  84.9 22.0 %all-to-all-start = ((bf16[12,96,128]{2,0,1:T(8,128)(2,1)}), bf16[12,96,128]{2,0,1:T(8,128)(2,1)S(1)}, u32[]{:S(2)}, u32[]{:S(2)}) async-start(bf16[12,96,128]{2,0,1:T(8,128)(2,1)} %copy.49), calls=%async_computation | async-start | bytes 786432 | tf_op jit(solution)/shard_map/all_to_all | solution.py:83
  88.4 111.4 %all-gather.8.cloned.1.call-start = ((), (), s32[]{:S(2)}) async-start(), calls=%async_computation.3 | async-start | bytes 2654208 | tf_op jit(solution)/shard_map/all_gather | solution.py:106
  141.2 4.9 %copy-start.18 = (bf16[128,128]{1,0:T(8,128)(2,1)S(1)}, bf16[128,128]{1,0:T(8,128)(2,1)}, u32[]{:S(2)}) copy-start(bf16[128,128]{1,0:T(8,128)(2,1)} %param.29) | copy-start | bytes 98308
  141.2 4.9 %copy-start.21 = (f32[128]{0:T(128)S(1)}, f32[128]{0:T(128)}, u32[]{:S(2)}) copy-start(f32[128]{0:T(128)} %param.28) | copy-start | bytes 1540
  144.2 1.9 copy-start.4
  144.2 1.9 copy-start.7
  146.2 3.2 copy-start.11
  146.9 3.7 %copy-start.10 = (bf16[12,96,128]{2,1,0:T(8,128)(2,1)S(1)}, bf16[12,96,128]{2,1,0:T(8,128)(2,1)}, u32[]{:S(2)}) copy-start(bf16[12,96,128]{2,1,0:T(8,128)(2,1)} %copy-done.9) | copy-start | bytes 884740
  147.7 5.9 %copy-start.15 = (bf16[12,96,128]{2,1,0:T(8,128)(2,1)S(1)}, bf16[12,96,128]{2,1,0:T(8,128)(2,1)}, u32[]{:S(2)}) copy-start(bf16[12,96,128]{2,1,0:T(8,128)(2,1)} %copy-done.14) | copy-start | bytes 884740
  149.2 139.7 %all-reduce.10.cloned.1.call-start = ((), (), s32[]{:S(2)}) async-start(), calls=%async_computation.5 | async-start | bytes 133120 | tf_op jit(solution)/shard_map/psum | solution.py:119
  218.3 2.5 copy-start.8
  220.2 143.0 %all-reduce.8.cloned.1.call-start = ((), (), s32[]{:S(2)}) async-start(), calls=%async_computation.4 | async-start | bytes 262144 | tf_op jit(solution)/shard_map/psum | solution.py:118
  (8 other events, 8.0 us)
Sparse Core Ops, SparseCore 0:
  17.1 54.5 all-gather.3
  84.1 53.5 all-gather.5
  149.3 50.4 all-gather.7
  220.3 68.4 all-reduce.9
  292.6 70.4 all-reduce.7
where the time goes:
time: 372 us; the launch traced here: 371 us
  waiting for transfers between devices  279 us (75%)
  local copies, waits for them, and re-layouts  27.9 us (8%)
  matrix products  23.6 us (6%)
  other arithmetic  22.7 us (6%)
  between operations  14.2 us (4%)
  starting transfers between devices  3.84 us (1%)
    psum x1, waiting for transfers between devices, shards(): lax.psum(grad_proj.astype(jnp.bfloat16), 'dap').astype(jnp.float32)  69.3 us
    psum x1, waiting for transfers between devices, shards(): lax.psum(grad_gate.astype(jnp.bfloat16), 'dap').astype(jnp.float32)  66.6 us
    all_gather x1, waiting for transfers between devices, shards(): lax.all_gather(right_b, 'dap', axis=0, tiled=True)  51.8 us
    all_gather x1, waiting for transfers between devices, shards(): shard_rows = lax.all_gather(grad_x_b, 'dap', axis=0, tiled=True)  44.1 us
    all_gather x1, waiting for transfers between devices, shards(): lax.all_gather(right_ib, 'dap', axis=0, tiled=True)  29.5 us
    all_to_all x1, waiting for transfers between devices, shards(): lax.all_to_all(left_ib, 'dap', split_axis=1, concat_axis=0, tiled=True)  17.3 us
  transfers between devices with their start and end apart: 6, of which 6 were waited for; matrix products, arithmetic and copies ran while one was open for 5% of the time, Pallas kernels for 0%

commit v1 on v0

v1 whole, which is shorter than its diff:
```python
import functools

import jax
import jax.numpy as jnp
from jax import lax
from jax.experimental import pallas as pl
from jax.experimental.pallas import tpu as pltpu
from jax.sharding import PartitionSpec as P

F32 = jnp.float32
BF16 = jnp.bfloat16
LANES = 128
A_OUT, B_OUT, X_OUT, A_IN, B_IN, X_IN, G_X, G_A, G_B, P_SUM, P_ALL = range(11)


def tn(w, x):
    return lax.dot_general(w, x, (((0,), (0,)), ((), ())), preferred_element_type=F32)


def nn(w, x):
    return jnp.dot(w, x, preferred_element_type=F32)


def nt(w, x):
    return lax.dot_general(w, x, (((1,), (1,)), ((), ())), preferred_element_type=F32)


def sigmoid(v):
    return 1.0 / (1.0 + jnp.exp(-v))


def norm_stats(v):
    centred = v - jnp.mean(v, axis=0, keepdims=True)
    inv = lax.rsqrt(jnp.mean(centred * centred, axis=0, keepdims=True) + 1e-05)
    return centred * inv, inv


def norm_back(grad, hat, inv, gain):
    scaled = grad * gain
    m1 = jnp.mean(scaled, axis=0, keepdims=True)
    m2 = jnp.mean(scaled * hat, axis=0, keepdims=True)
    return inv * (scaled - m1 - hat * m2)


def lane_sum(v):
    return jnp.sum(v, axis=1, keepdims=True)


def kernel(
    n, rows, res, lc,
    pair, cot, masks, params, out_proj, out_gate, out_final, in_proj, in_gate, in_final,
    grad_out, gp_out, gg_out, gf_out, gains_out,
    cols, start, normed, gate, in_p, cot_t, mid, logit_s, gv, gy, gl,
    a_s, b_s, x_s, a_r, b_r, x_r,
    a2_s, b2_s, x2_s, a2_r, b2_r, x2_r,
    gx_s, gx_r, ga_s, gb_s, ga_r, gb_r,
    slab_a, slab_b, slab_o, slab_p, mat_a, mat_b,
    acc_p, acc_g, acc_f, acc_n, acc_m, g_s, g_r, t_s, t_r,
    send_sem, recv_sem,
):
    me = lax.axis_index("dap")
    c = start.shape[0]
    per = c // n
    total = rows * res
    chunks = total // lc
    tiles = -(-res // LANES)
    inv_count = 1.0 / res

    barrier = pltpu.get_barrier_semaphore()
    for p in range(1, n):
        pl.semaphore_signal(
            barrier, inc=1, device_id={"dap": lax.rem(me + p, n)},
            device_id_type=pl.DeviceIdType.MESH,
        )
    pl.semaphore_wait(barrier, n - 1)

    def copy_to(which, src, dst, peer):
        return pltpu.make_async_remote_copy(
            src_ref=src, dst_ref=dst,
            send_sem=send_sem.at[which, peer], recv_sem=recv_sem.at[which, me],
            device_id={"dap": peer}, device_id_type=pl.DeviceIdType.MESH,
        )

    def spread(which, src, dst):
        for p in range(1, n):
            peer = lax.rem(me + p, n)
            copy_to(which, src.at[peer], dst.at[me], peer).start()
        dst[me] = src[me]

    def collect(which, src, dst):
        for p in range(1, n):
            peer = lax.rem(me + n - p, n)
            pltpu.make_async_remote_copy(
                src_ref=src.at[peer], dst_ref=dst.at[peer],
                send_sem=send_sem.at[which, peer], recv_sem=recv_sem.at[which, peer],
                device_id={"dap": peer}, device_id_type=pl.DeviceIdType.MESH,
            ).wait()

    def lanes_of(k):
        return pl.ds(pl.multiple_of(k * lc, lc), lc)

    def put(ref, ds, value):
        ref[:, :, ds] = value.reshape(n, per, lc).astype(BF16)

    def take(ref, ds):
        return ref[:, :, ds].astype(F32).reshape(c, lc)

    def to_slab(ref, slab):
        def one(s, _):
            block = ref[s].astype(F32)
            for i in range(rows):
                part = block[:, i * res : (i + 1) * res]
                at = pl.ds(pl.multiple_of((s * rows + i) * per, per), per)
                for t in range(tiles):
                    width = min(LANES, res - t * LANES)
                    slab[t, at, :width] = part[:, t * LANES : t * LANES + width]
            return 0

        lax.fori_loop(0, n, one, 0)

    def matrix(slab, ch):
        parts = [slab[t, pl.ds(ch, res, stride=per), :] for t in range(tiles)]
        whole = parts[0] if tiles == 1 else jnp.concatenate(parts, axis=1)
        return whole[:, :res].astype(BF16)

    def keep(slab, ch, value):
        pad = tiles * LANES - res
        if pad:
            value = jnp.concatenate([value, jnp.zeros((res, pad), F32)], axis=1)
        for t in range(tiles):
            slab[t, pl.ds(ch, res, stride=per), :] = value[:, t * LANES : (t + 1) * LANES]

    def from_slab(slab, ref):
        def one(s, _):
            parts = []
            for i in range(rows):
                at = pl.ds(pl.multiple_of((s * rows + i) * per, per), per)
                for t in range(tiles):
                    width = min(LANES, res - t * LANES)
                    parts.append(slab[t, at, :width])
            ref[s] = jnp.concatenate(parts, axis=1).astype(BF16)
            return 0

        lax.fori_loop(0, n, one, 0)

    cols[...] = params[...].T
    emb0, emb1 = cols[:, 0:1], cols[:, 1:2]
    g_on, g_om, g_in, g_im = (cols[:, q : q + 1] for q in range(2, 6))

    @pl.loop(0, chunks)
    def _(k):
        ds = lanes_of(k)
        same = masks[1:2, ds] > 0.5
        x = pair[ds, :].astype(F32).T + jnp.where(same, emb1, emb0)
        start[:, ds] = x
        hat, _ = norm_stats(x)
        nb = (hat * g_on).astype(BF16)
        normed[:, ds] = nb
        p = tn(out_proj[...], nb)
        pm = masks[0:1, ds]
        put(a_s, ds, pm * sigmoid(p[:c]) * p[c : 2 * c])
        put(b_s, ds, pm * sigmoid(p[2 * c : 3 * c]) * p[3 * c :])

    spread(A_OUT, a_s, a_r)
    spread(B_OUT, b_s, b_r)

    @pl.loop(0, chunks)
    def _(k):
        ds = lanes_of(k)
        gate[:, ds] = sigmoid(tn(out_gate[...], normed[:, ds]))
        cot_t[:, ds] = cot[ds, :].astype(F32).T

    collect(A_OUT, a_s, a_r)
    to_slab(a_r, slab_a)
    collect(B_OUT, b_s, b_r)
    to_slab(b_r, slab_b)
    for ch in range(per):
        keep(slab_o, ch, nt(matrix(slab_a, ch), matrix(slab_b, ch)))
    from_slab(slab_o, x_s)
    spread(X_OUT, x_s, x_r)
    collect(X_OUT, x_s, x_r)

    @pl.loop(0, chunks)
    def _(k):
        ds = lanes_of(k)
        hat, _ = norm_stats(take(x_r, ds))
        y = (hat * g_om).astype(BF16)
        m = (start[:, ds] + gate[:, ds] * tn(out_final[...], y)).astype(BF16)
        mid[:, ds] = m
        hat, _ = norm_stats(m.astype(F32))
        nb = (hat * g_in).astype(BF16)
        normed[:, ds] = nb
        p = tn(in_proj[...], nb)
        in_p[:, ds] = p
        pm = masks[0:1, ds]
        put(a2_s, ds, pm * sigmoid(p[:c]) * p[c : 2 * c])
        put(b2_s, ds, pm * sigmoid(p[2 * c : 3 * c]) * p[3 * c :])

    spread(A_IN, a2_s, a2_r)
    spread(B_IN, b2_s, b2_r)

    @pl.loop(0, chunks)
    def _(k):
        ds = lanes_of(k)
        s = sigmoid(tn(in_gate[...], normed[:, ds]))
        logit_s[:, ds] = s
        v = (cot_t[:, ds] * s).astype(BF16)
        gv[:, ds] = v
        gy[:, ds] = nn(in_final[...], v)

    acc_p[...] = jnp.zeros_like(acc_p)
    acc_g[...] = jnp.zeros_like(acc_g)
    acc_f[...] = jnp.zeros_like(acc_f)
    acc_n[...] = jnp.zeros_like(acc_n)
    acc_m[...] = jnp.zeros_like(acc_m)

    collect(A_IN, a2_s, a2_r)
    to_slab(a2_r, slab_a)
    collect(B_IN, b2_s, b2_r)
    to_slab(b2_r, slab_b)
    for ch in range(per):
        a = matrix(slab_a, ch)
        b = matrix(slab_b, ch)
        mat_a[ch] = a
        mat_b[ch] = b
        keep(slab_o, ch, tn(a, b))
    from_slab(slab_o, x2_s)
    spread(X_IN, x2_s, x2_r)
    collect(X_IN, x2_s, x2_r)

    @pl.loop(0, chunks)
    def _(k):
        ds = lanes_of(k)
        hat, inv = norm_stats(take(x2_r, ds))
        y = (hat * g_im).astype(BF16)
        value = tn(in_final[...], y)
        s = logit_s[:, ds]
        grad_l = (cot_t[:, ds] * value * s * (1.0 - s)).astype(BF16)
        gl[:, ds] = grad_l
        g = gy[:, ds]
        acc_m[...] += lane_sum(g * hat)
        put(gx_s, ds, norm_back(g, hat, inv, g_im))
        acc_f[...] += nt(y, gv[:, ds])

    spread(G_X, gx_s, gx_r)

    @pl.loop(0, chunks)
    def _(k):
        ds = lanes_of(k)
        grad_l = gl[:, ds]
        acc_g[...] += nt(normed[:, ds], grad_l)
        gy[:, ds] = nn(in_gate[...], grad_l)

    collect(G_X, gx_s, gx_r)
    to_slab(gx_r, slab_a)
    for ch in range(per):
        gx = matrix(slab_a, ch)
        keep(slab_o, ch, nt(mat_b[ch], gx))
        keep(slab_p, ch, nn(mat_a[ch], gx))
    from_slab(slab_o, ga_s)
    spread(G_A, ga_s, ga_r)
    from_slab(slab_p, gb_s)
    spread(G_B, gb_s, gb_r)
    collect(G_A, ga_s, ga_r)
    collect(G_B, gb_s, gb_r)

    @pl.loop(0, chunks)
    def _(k):
        ds = lanes_of(k)
        pm = masks[0:1, ds]
        s0 = sigmoid(in_p[:c, ds])
        s2 = sigmoid(in_p[2 * c : 3 * c, ds])
        ga = take(ga_r, ds) * pm * s0
        gb = take(gb_r, ds) * pm * s2
        q0 = (ga * in_p[c : 2 * c, ds] * (1.0 - s0)).astype(BF16)
        q2 = (gb * in_p[3 * c :, ds] * (1.0 - s2)).astype(BF16)
        q = jnp.concatenate([q0, ga.astype(BF16), q2, gb.astype(BF16)], axis=0)
        acc_p[...] += nt(normed[:, ds], q)
        g = nn(in_proj[...], q) + gy[:, ds]
        hat, inv = norm_stats(mid[:, ds].astype(F32))
        acc_n[...] += lane_sum(g * hat)
        z = cot_t[:, ds] + norm_back(g, hat, inv, g_in)
        grad_out[ds, :] = z.T.astype(BF16)

    lane = lax.broadcasted_iota(jnp.int32, (c, LANES), 1)
    gains = jnp.where(lane == 0, acc_n[...], jnp.where(lane == 1, acc_m[...], 0.0))
    whole = jnp.concatenate([acc_p[...], acc_g[...], acc_f[...], gains], axis=1) * inv_count
    g_s[...] = whole.reshape(n, per, whole.shape[1]).astype(BF16)
    spread(P_SUM, g_s, g_r)
    collect(P_SUM, g_s, g_r)
    summed = jnp.sum(g_r[...].astype(F32), axis=0).astype(BF16)
    t_s[...] = summed
    for p in range(1, n):
        peer = lax.rem(me + p, n)
        copy_to(P_ALL, t_s, t_r.at[me], peer).start()
    t_r[me] = summed
    for p in range(1, n):
        peer = lax.rem(me + n - p, n)
        pltpu.make_async_remote_copy(
            src_ref=t_s, dst_ref=t_r.at[peer],
            send_sem=send_sem.at[P_ALL, peer], recv_sem=recv_sem.at[P_ALL, peer],
            device_id={"dap": peer}, device_id_type=pl.DeviceIdType.MESH,
        ).wait()
    final = t_r[...].astype(F32).reshape(c, t_r.shape[2])
    gp_out[...] = final[:, : 4 * c]
    gg_out[...] = final[:, 4 * c : 5 * c]
    gf_out[...] = final[:, 5 * c : 6 * c]
    gains_out[...] = final[:, 6 * c :].T[:8]


def shards(n, pair, cotangent, residue_mask, chain_ids, chain_embed, out_norm_gain, out_proj,
           out_gate, out_mid_gain, out_final, in_norm_gain, in_proj, in_gate, in_mid_gain, in_final):
    rows, res, c = pair.shape
    total = rows * res
    per = c // n
    lc = max(q for q in range(LANES, 3 * LANES + 1, LANES) if total % q == 0)
    tiles = -(-res // LANES)
    row_start = lax.axis_index("dap") * rows
    row_mask = lax.dynamic_slice_in_dim(residue_mask, row_start, rows, 0)
    row_chain = lax.dynamic_slice_in_dim(chain_ids, row_start, rows, 0)
    pair_mask = (row_mask[:, None] * residue_mask[None, :]).astype(F32)
    same = (row_chain[:, None] == chain_ids[None, :]).astype(F32)
    masks = jnp.stack([pair_mask.reshape(total), same.reshape(total)])
    params = jnp.concatenate(
        [chain_embed, jnp.stack([out_norm_gain, out_mid_gain, in_norm_gain, in_mid_gain]),
         jnp.zeros((2, c), F32)], axis=0)

    def full(dtype):
        return pltpu.VMEM((c, total), dtype)

    swap = pltpu.VMEM((n, per, total), BF16)
    slab = pltpu.VMEM((tiles, res * per, LANES), F32)
    mats = pltpu.VMEM((per, res, res), BF16)
    wide = 6 * c + LANES
    scratch = [
        pltpu.VMEM((c, 8), F32), full(F32), full(BF16), full(F32),
        pltpu.VMEM((4 * c, total), F32), full(F32), full(BF16), full(F32), full(BF16), full(F32),
        full(BF16),
    ] + [swap] * 18 + [slab] * 4 + [mats] * 2 + [
        pltpu.VMEM((c, 4 * c), F32), pltpu.VMEM((c, c), F32), pltpu.VMEM((c, c), F32),
        pltpu.VMEM((c, 1), F32), pltpu.VMEM((c, 1), F32),
        pltpu.VMEM((n, per, wide), BF16), pltpu.VMEM((n, per, wide), BF16),
        pltpu.VMEM((per, wide), BF16), pltpu.VMEM((n, per, wide), BF16),
        pltpu.SemaphoreType.DMA((11, n)), pltpu.SemaphoreType.DMA((11, n)),
    ]
    vmem = pl.BlockSpec(memory_space=pltpu.VMEM)
    grad, gp, gg, gf, gains = pl.pallas_call(
        functools.partial(kernel, n, rows, res, lc),
        out_shape=(
            jax.ShapeDtypeStruct((total, c), BF16),
            jax.ShapeDtypeStruct((c, 4 * c), F32),
            jax.ShapeDtypeStruct((c, c), F32),
            jax.ShapeDtypeStruct((c, c), F32),
            jax.ShapeDtypeStruct((8, c), F32),
        ),
        in_specs=[vmem] * 10,
        out_specs=(vmem,) * 5,
        scratch_shapes=scratch,
        compiler_params=pltpu.CompilerParams(
            collective_id=0, has_side_effects=True, vmem_limit_bytes=60 * 1024 * 1024
        ),
    )(
        pair.reshape(total, c), cotangent.reshape(total, c), masks, params,
        out_proj, out_gate, out_final, in_proj, in_gate, in_final,
    )
    return grad.reshape(rows, res, c), gp, gg, gf, gains[0], gains[1]


def solution(mesh):
    split = P("dap", "cplx", None)
    return jax.shard_map(
        functools.partial(shards, mesh.shape["dap"]),
        mesh=mesh,
        in_specs=(split, split, P("cplx"), P("cplx")) + (P(),) * 11,
        out_specs=(split, P("cplx", None), P("cplx", None), P("cplx", None), P("cplx"), P("cplx")),
        check_vma=False,
    )
```

time: 372 us -> 105 us (0.28)
  waiting for transfers between devices: 279 us -> 0 us
  Pallas kernels: 0 us -> 95.4 us
  matrix products: 23.6 us -> 0 us
  other arithmetic: 22.7 us -> 0.76 us
  local copies, waits for them, and re-layouts: 27.9 us -> 8.22 us
  between operations: 14.2 us -> 0.69 us
  starting transfers between devices: 3.84 us -> 0 us
    psum x2 -> x0, waiting for transfers between devices: 136 us -> none  [the longest x1 69.3 us: shards(): lax.psum(grad_proj.astype(jnp.bfloat16), 'dap').astype(jnp.float32)]
    all_gather x3 -> x0, waiting for transfers between devices: 125 us -> none  [the longest x1 51.8 us: shards(): lax.all_gather(right_b, 'dap', axis=0, tiled=True)]
    pallas_call x0 -> x1, Pallas kernels: none -> 95.4 us  [shards(): pl.pallas_call(functools.partial(kernel, n, rows, res, lc), out_shape=(ja...]
    dot_general x16 -> x0, matrix products: 23.6 us -> none  [the longest x1 3.76 us: shards(): jnp.einsum('kjc,ijc->kic', right_ib, shard_rows, preferred_element_type=f32)]
    all_to_all x1 -> x0, waiting for transfers between devices: 17.3 us -> none  [shards(): lax.all_to_all(left_ib, 'dap', split_axis=1, concat_axis=0, tiled=True)]
    convert_element_type x14 -> x2, other arithmetic: 14 us -> 0.15 us  [the longest x1 0.08 us: shards(): pair_mask = (row_mask[:, None] * residue_mask[None, :]).astype(F32)]
    all_gather x3 -> x0, local copies, waits for them, and re-layouts: 10.6 us -> none  [the longest x1 3.53 us: shards(): lax.all_gather(right_b, 'dap', axis=0, tiled=True)]
    dot_general x3 -> x0, local copies, waits for them, and re-layouts: 5.51 us -> none  [the longest x1 2.36 us: shards(): jnp.einsum('kjc,ijc->kic', right_ib, shard_rows, preferred_element_type=f32)]
  transfers between devices with their start and end apart: 6 -> 0, of which waited for: 6 -> 0; matrix products, arithmetic and copies ran while one was open for 5% -> 0% of each run, Pallas kernels for 0% -> 0%
where the time goes in v1:
time: 105 us
  Pallas kernels  95.4 us (91%)
  local copies, waits for them, and re-layouts  8.22 us (8%)
    pallas_call x1, Pallas kernels, shards(): pl.pallas_call(functools.partial(kernel, n, rows, res, lc), out_shape=(ja...  95.4 us
    unnamed x24, local copies, waits for them, and re-layouts  6.02 us

profile of v1, /device:TPU:0, one launch (start us, length us, event | category | flops | bytes accessed | tf_op | source)
XLA Modules:
  0.0 105.1 jit_solution(6643141804203625616)
XLA Ops:
  0.6 0.6 copy-done.4
  1.3 0.1 dynamic_slice.6
  1.4 0.1 multiply_convert_fusion
  1.4 0.1 convert_element_type.27
  1.5 0.6 copy-done.5
  2.1 0.1 dynamic_slice.7
  2.2 0.1 compare_convert_fusion
  2.2 0.1 reshape.81
  2.3 0.6 pad_maximum_fusion.masks
  3.0 0.0 copy-start.6
  3.0 0.6 copy-done.7
  3.6 0.0 copy-done.8
  3.6 0.0 copy-done.9
  3.6 0.0 copy-done.3
  3.7 0.0 copy-done.6
  3.7 0.6 concatenate.3.params
  4.3 95.4 %shard_map.190 = (bf16[1152,128]{1,0:T(8,128)(2,1)}, f32[128,512]{1,0:T(8,128)}, f32[128,128]{1,0:T(8,128)}, f32[128,128]{1,0:T(8,128)}, f32[8,128]{1,0:T(8,128)}) custom-call(bf16[1152,128]{1,0:T(8,128)(2,1)} %bitcast.11, bf16[1152,128]{1,0:T(8,128)(2,1)} %bitcast.12, f32[2,1152]{1,0:T(2,128)} %pad_maximum_fusion.masks, f32[8,128]{1,0:T(8,128)} %concatenate.3.params, ...), custom_call_target="tpu_custom_call" | custom-call | tf_op jit(solution)/shard_map/pallas_call | solution.py:347
  99.7 1.3 %slice_bitcast_fusion = (f32[128]{0:T(128)}, f32[128]{0:T(128)}) fusion(f32[8,128]{1,0:T(8,128)} %get-tuple-element.15), kind=kLoop, calls=%fused_computation.3 | loop fusion | bytes 2048 | tf_op jit(solution)/shard_map/squeeze | solution.py:366
  101.0 1.7 %copy.25 = bf16[12,96,128]{2,1,0:T(8,128)(2,1)} copy(bf16[12,96,128]{2,1,0:T(8,128)(2,1)} %bitcast.13) | data formatting | bytes 589824
  102.8 0.7 copy.26
  103.5 0.2 copy-done.2
  103.6 0.6 copy.27
  104.3 0.2 copy-done.1
  104.5 0.6 copy.28
  (11 shorter events, 0.0 us)
Async XLA Ops:
  0.6 0.7 copy-start.4
  1.4 0.7 copy-start.5
  2.9 0.7 copy-start.7
  2.9 0.7 copy-start.8
  3.0 0.7 copy-start.9
  3.0 0.7 copy-start.3
  3.0 0.7 copy-start.6
  101.0 1.7 %copy-start = (f32[128,512]{1,0:T(8,128)S(1)}, f32[128,512]{1,0:T(8,128)}, u32[]{:S(2)}) copy-start(f32[128,512]{1,0:T(8,128)} %get-tuple-element.25) | copy-start | bytes 786436
  102.8 0.9 copy-start.2
  103.6 0.9 copy-start.1

commit v2 on v1

--- a/solution.py
+++ b/solution.py
@@ -10,7 +10,7 @@
 F32 = jnp.float32
 BF16 = jnp.bfloat16
 LANES = 128
-A_OUT, B_OUT, X_OUT, A_IN, B_IN, X_IN, G_X, G_A, G_B, P_SUM, P_ALL = range(11)
+A_OUT, B_OUT, X_OUT, A_IN, B_IN, X_IN, G_X, G_A, G_B, P_SUM, P_ALL, H_SUM, H_ALL = range(13)
 
 
 def tn(w, x):
@@ -55,7 +55,7 @@
     a2_s, b2_s, x2_s, a2_r, b2_r, x2_r,
     gx_s, gx_r, ga_s, gb_s, ga_r, gb_r,
     slab_a, slab_b, slab_o, slab_p, mat_a, mat_b,
-    acc_p, acc_g, acc_f, acc_n, acc_m, g_s, g_r, t_s, t_r,
+    acc_p, acc_g, acc_f, acc_n, acc_m, g_s, g_r, t_s, t_r, h_s, h_r, u_s, u_r,
     send_sem, recv_sem,
 ):
     me = lax.axis_index("dap")
@@ -63,6 +63,7 @@
     per = c // n
     total = rows * res
     chunks = total // lc
+    crows = lc // res
     tiles = -(-res // LANES)
     inv_count = 1.0 / res
 
@@ -74,27 +75,29 @@
         )
     pl.semaphore_wait(barrier, n - 1)
 
-    def copy_to(which, src, dst, peer):
+    def copy_to(sem, src, dst, peer):
         return pltpu.make_async_remote_copy(
-            src_ref=src, dst_ref=dst,
-            send_sem=send_sem.at[which, peer], recv_sem=recv_sem.at[which, me],
+            src_ref=src, dst_ref=dst, send_sem=send_sem.at[sem], recv_sem=recv_sem.at[sem],
             device_id={"dap": peer}, device_id_type=pl.DeviceIdType.MESH,
         )
 
-    def spread(which, src, dst):
+    def spread(which, src, dst, k=0, ds=None):
+        def view(ref, at):
+            return ref.at[at] if ds is None else ref.at[at, :, ds]
+
         for p in range(1, n):
             peer = lax.rem(me + p, n)
-            copy_to(which, src.at[peer], dst.at[me], peer).start()
-        dst[me] = src[me]
-
-    def collect(which, src, dst):
-        for p in range(1, n):
-            peer = lax.rem(me + n - p, n)
-            pltpu.make_async_remote_copy(
-                src_ref=src.at[peer], dst_ref=dst.at[peer],
-                send_sem=send_sem.at[which, peer], recv_sem=recv_sem.at[which, peer],
-                device_id={"dap": peer}, device_id_type=pl.DeviceIdType.MESH,
-            ).wait()
+            copy_to(which * chunks + k, view(src, peer), view(dst, me), peer).start()
+        if ds is None:
+            dst[me] = src[me]
+        else:
+            dst[me, :, ds] = src[me, :, ds]
+
+    def collect(which, src, dst, k=0, ds=None):
+        def view(ref):
+            return ref.at[pl.ds(0, n - 1)] if ds is None else ref.at[pl.ds(0, n - 1), :, ds]
+
+        copy_to(which * chunks + k, view(src), view(dst), lax.rem(me + 1, n)).wait()
 
     def lanes_of(k):
         return pl.ds(pl.multiple_of(k * lc, lc), lc)
@@ -105,43 +108,57 @@
     def take(ref, ds):
         return ref[:, :, ds].astype(F32).reshape(c, lc)
 
-    def to_slab(ref, slab):
-        def one(s, _):
-            block = ref[s].astype(F32)
-            for i in range(rows):
+    def to_slab(ref, slab, k, by_chunk=False):
+        for s in range(n):
+            block = ref[s, :, lanes_of(k)].astype(F32)
+            row = (k * n + s) * crows if by_chunk else s * rows + k * crows
+            for i in range(crows):
                 part = block[:, i * res : (i + 1) * res]
-                at = pl.ds(pl.multiple_of((s * rows + i) * per, per), per)
+                at = pl.ds(pl.multiple_of((row + i) * per, per), per)
                 for t in range(tiles):
                     width = min(LANES, res - t * LANES)
                     slab[t, at, :width] = part[:, t * LANES : t * LANES + width]
-            return 0
-
-        lax.fori_loop(0, n, one, 0)
-
-    def matrix(slab, ch):
-        parts = [slab[t, pl.ds(ch, res, stride=per), :] for t in range(tiles)]
+
+    def matrix(slab, ch, first=0, count=res):
+        at = pl.ds(first * per + ch, count, stride=per)
+        parts = [slab[t, at, :] for t in range(tiles)]
         whole = parts[0] if tiles == 1 else jnp.concatenate(parts, axis=1)
         return whole[:, :res].astype(BF16)
 
-    def keep(slab, ch, value):
+    def keep(slab, ch, value, first=0):
+        count = value.shape[0]
         pad = tiles * LANES - res
         if pad:
-            value = jnp.concatenate([value, jnp.zeros((res, pad), F32)], axis=1)
+            value = jnp.concatenate([value, jnp.zeros((count, pad), F32)], axis=1)
         for t in range(tiles):
-            slab[t, pl.ds(ch, res, stride=per), :] = value[:, t * LANES : (t + 1) * LANES]
-
-    def from_slab(slab, ref):
-        def one(s, _):
+            at = pl.ds(first * per + ch, count, stride=per)
+            slab[t, at, :] = value[:, t * LANES : (t + 1) * LANES]
+
+    def from_slab(slab, ref, k, by_chunk=False):
+        for s in range(n):
+            row = (k * n + s) * crows if by_chunk else s * rows + k * crows
             parts = []
-            for i in range(rows):
-                at = pl.ds(pl.multiple_of((s * rows + i) * per, per), per)
+            for i in range(crows):
+                at = pl.ds(pl.multiple_of((row + i) * per, per), per)
                 for t in range(tiles):
                     width = min(LANES, res - t * LANES)
                     parts.append(slab[t, at, :width])
-            ref[s] = jnp.concatenate(parts, axis=1).astype(BF16)
-            return 0
-
-        lax.fori_loop(0, n, one, 0)
+            ref[s, :, lanes_of(k)] = jnp.concatenate(parts, axis=1).astype(BF16)
+
+    def early():
+        return jnp.concatenate([acc_g[...], acc_f[...]], axis=1) * inv_count
+
+    def hand_round(which, src, mine, dst):
+        summed = jnp.sum(src[...].astype(F32), axis=0).astype(BF16)
+        mine[...] = summed
+        for p in range(1, n):
+            copy_to(which * chunks, mine, dst.at[me], lax.rem(me + p, n)).start()
+        dst[me] = summed
+
+    def gathered(which, dst):
+        block = dst.at[pl.ds(0, n - 1)]
+        copy_to(which * chunks, block, block, lax.rem(me + 1, n)).wait()
+        return dst[...].astype(F32).reshape(c, dst.shape[2])
 
     cols[...] = params[...].T
     emb0, emb1 = cols[:, 0:1], cols[:, 1:2]
@@ -160,9 +177,11 @@
         pm = masks[0:1, ds]
         put(a_s, ds, pm * sigmoid(p[:c]) * p[c : 2 * c])
         put(b_s, ds, pm * sigmoid(p[2 * c : 3 * c]) * p[3 * c :])
-
-    spread(A_OUT, a_s, a_r)
-    spread(B_OUT, b_s, b_r)
+        spread(B_OUT, b_s, b_r, k, ds)
+
+    @pl.loop(0, chunks)
+    def _(k):
+        spread(A_OUT, a_s, a_r, k, lanes_of(k))
 
     @pl.loop(0, chunks)
     def _(k):
@@ -170,19 +189,30 @@
         gate[:, ds] = sigmoid(tn(out_gate[...], normed[:, ds]))
         cot_t[:, ds] = cot[ds, :].astype(F32).T
 
-    collect(A_OUT, a_s, a_r)
-    to_slab(a_r, slab_a)
-    collect(B_OUT, b_s, b_r)
-    to_slab(b_r, slab_b)
+    @pl.loop(0, chunks)
+    def _(k):
+        collect(B_OUT, b_s, b_r, k, lanes_of(k))
+        to_slab(b_r, slab_b, k)
+
     for ch in range(per):
-        keep(slab_o, ch, nt(matrix(slab_a, ch), matrix(slab_b, ch)))
-    from_slab(slab_o, x_s)
-    spread(X_OUT, x_s, x_r)
-    collect(X_OUT, x_s, x_r)
-
-    @pl.loop(0, chunks)
-    def _(k):
-        ds = lanes_of(k)
+        mat_b[ch] = matrix(slab_b, ch)
+
+    group = n * crows
+
+    @pl.loop(0, chunks)
+    def _(k):
+        ds = lanes_of(k)
+        collect(A_OUT, a_s, a_r, k, ds)
+        to_slab(a_r, slab_a, k, True)
+        for ch in range(per):
+            keep(slab_o, ch, nt(matrix(slab_a, ch, k * group, group), mat_b[ch]), k * group)
+        from_slab(slab_o, x_s, k, True)
+        spread(X_OUT, x_s, x_r, k, ds)
+
+    @pl.loop(0, chunks)
+    def _(k):
+        ds = lanes_of(k)
+        collect(X_OUT, x_s, x_r, k, ds)
         hat, _ = norm_stats(take(x_r, ds))
         y = (hat * g_om).astype(BF16)
         m = (start[:, ds] + gate[:, ds] * tn(out_final[...], y)).astype(BF16)
@@ -195,9 +225,8 @@
         pm = masks[0:1, ds]
         put(a2_s, ds, pm * sigmoid(p[:c]) * p[c : 2 * c])
         put(b2_s, ds, pm * sigmoid(p[2 * c : 3 * c]) * p[3 * c :])
-
-    spread(A_IN, a2_s, a2_r)
-    spread(B_IN, b2_s, b2_r)
+        spread(A_IN, a2_s, a2_r, k, ds)
+        spread(B_IN, b2_s, b2_r, k, ds)
 
     @pl.loop(0, chunks)
     def _(k):
@@ -214,23 +243,29 @@
     acc_n[...] = jnp.zeros_like(acc_n)
     acc_m[...] = jnp.zeros_like(acc_m)
 
-    collect(A_IN, a2_s, a2_r)
-    to_slab(a2_r, slab_a)
-    collect(B_IN, b2_s, b2_r)
-    to_slab(b2_r, slab_b)
+    @pl.loop(0, chunks)
+    def _(k):
+        collect(A_IN, a2_s, a2_r, k, lanes_of(k))
+        to_slab(a2_r, slab_a, k)
+        collect(B_IN, b2_s, b2_r, k, lanes_of(k))
+        to_slab(b2_r, slab_b, k)
+
     for ch in range(per):
         a = matrix(slab_a, ch)
         b = matrix(slab_b, ch)
         mat_a[ch] = a
         mat_b[ch] = b
         keep(slab_o, ch, tn(a, b))
-    from_slab(slab_o, x2_s)
-    spread(X_IN, x2_s, x2_r)
-    collect(X_IN, x2_s, x2_r)
-
-    @pl.loop(0, chunks)
-    def _(k):
-        ds = lanes_of(k)
+
+    @pl.loop(0, chunks)
+    def _(k):
+        from_slab(slab_o, x2_s, k)
+        spread(X_IN, x2_s, x2_r, k, lanes_of(k))
+
+    @pl.loop(0, chunks)
+    def _(k):
+        ds = lanes_of(k)
+        collect(X_IN, x2_s, x2_r, k, ds)
         hat, inv = norm_stats(take(x2_r, ds))
         y = (hat * g_im).astype(BF16)
         value = tn(in_final[...], y)
@@ -240,9 +275,8 @@
         g = gy[:, ds]
         acc_m[...] += lane_sum(g * hat)
         put(gx_s, ds, norm_back(g, hat, inv, g_im))
+        spread(G_X, gx_s, gx_r, k, ds)
         acc_f[...] += nt(y, gv[:, ds])
-
-    spread(G_X, gx_s, gx_r)
 
     @pl.loop(0, chunks)
     def _(k):
@@ -251,22 +285,34 @@
         acc_g[...] += nt(normed[:, ds], grad_l)
         gy[:, ds] = nn(in_gate[...], grad_l)
 
-    collect(G_X, gx_s, gx_r)
-    to_slab(gx_r, slab_a)
+    h_s[...] = early().reshape(n, per, 2 * c).astype(BF16)
+    spread(H_SUM, h_s, h_r)
+
+    @pl.loop(0, chunks)
+    def _(k):
+        collect(G_X, gx_s, gx_r, k, lanes_of(k))
+        to_slab(gx_r, slab_a, k)
+
     for ch in range(per):
         gx = matrix(slab_a, ch)
         keep(slab_o, ch, nt(mat_b[ch], gx))
         keep(slab_p, ch, nn(mat_a[ch], gx))
-    from_slab(slab_o, ga_s)
-    spread(G_A, ga_s, ga_r)
-    from_slab(slab_p, gb_s)
-    spread(G_B, gb_s, gb_r)
-    collect(G_A, ga_s, ga_r)
-    collect(G_B, gb_s, gb_r)
-
-    @pl.loop(0, chunks)
-    def _(k):
-        ds = lanes_of(k)
+
+    @pl.loop(0, chunks)
+    def _(k):
+        from_slab(slab_o, ga_s, k)
+        spread(G_A, ga_s, ga_r, k, lanes_of(k))
+        from_slab(slab_p, gb_s, k)
+        spread(G_B, gb_s, gb_r, k, lanes_of(k))
+
+    collect(H_SUM, h_s, h_r)
+    hand_round(H_ALL, h_r, u_s, u_r)
+
+    @pl.loop(0, chunks)
+    def _(k):
+        ds = lanes_of(k)
+        collect(G_A, ga_s, ga_r, k, ds)
+        collect(G_B, gb_s, gb_r, k, ds)
         pm = masks[0:1, ds]
         s0 = sigmoid(in_p[:c, ds])
         s2 = sigmoid(in_p[2 * c : 3 * c, ds])
@@ -284,28 +330,17 @@
 
     lane = lax.broadcasted_iota(jnp.int32, (c, LANES), 1)
     gains = jnp.where(lane == 0, acc_n[...], jnp.where(lane == 1, acc_m[...], 0.0))
-    whole = jnp.concatenate([acc_p[...], acc_g[...], acc_f[...], gains], axis=1) * inv_count
+    whole = jnp.concatenate([acc_p[...], gains], axis=1) * inv_count
     g_s[...] = whole.reshape(n, per, whole.shape[1]).astype(BF16)
     spread(P_SUM, g_s, g_r)
+    both = gathered(H_ALL, u_r)
+    gg_out[...] = both[:, :c]
+    gf_out[...] = both[:, c:]
     collect(P_SUM, g_s, g_r)
-    summed = jnp.sum(g_r[...].astype(F32), axis=0).astype(BF16)
-    t_s[...] = summed
-    for p in range(1, n):
-        peer = lax.rem(me + p, n)
-        copy_to(P_ALL, t_s, t_r.at[me], peer).start()
-    t_r[me] = summed
-    for p in range(1, n):
-        peer = lax.rem(me + n - p, n)
-        pltpu.make_async_remote_copy(
-            src_ref=t_s, dst_ref=t_r.at[peer],
-            send_sem=send_sem.at[P_ALL, peer], recv_sem=recv_sem.at[P_ALL, peer],
-            device_id={"dap": peer}, device_id_type=pl.DeviceIdType.MESH,
-        ).wait()
-    final = t_r[...].astype(F32).reshape(c, t_r.shape[2])
+    hand_round(P_ALL, g_r, t_s, t_r)
+    final = gathered(P_ALL, t_r)
     gp_out[...] = final[:, : 4 * c]
-    gg_out[...] = final[:, 4 * c : 5 * c]
-    gf_out[...] = final[:, 5 * c : 6 * c]
-    gains_out[...] = final[:, 6 * c :].T[:8]
+    gains_out[...] = final[:, 4 * c :].T[:8]
 
 
 def shards(n, pair, cotangent, residue_mask, chain_ids, chain_embed, out_norm_gain, out_proj,
@@ -313,7 +348,10 @@
     rows, res, c = pair.shape
     total = rows * res
     per = c // n
-    lc = max(q for q in range(LANES, 3 * LANES + 1, LANES) if total % q == 0)
+    lc = res * min(
+        q for q in range(1, rows + 1)
+        if rows % q == 0 and q * res % LANES == 0 and (rows // q <= 3)
+    )
     tiles = -(-res // LANES)
     row_start = lax.axis_index("dap") * rows
     row_mask = lax.dynamic_slice_in_dim(residue_mask, row_start, rows, 0)
@@ -331,7 +369,7 @@
     swap = pltpu.VMEM((n, per, total), BF16)
     slab = pltpu.VMEM((tiles, res * per, LANES), F32)
     mats = pltpu.VMEM((per, res, res), BF16)
-    wide = 6 * c + LANES
+    wide = 4 * c + LANES
     scratch = [
         pltpu.VMEM((c, 8), F32), full(F32), full(BF16), full(F32),
         pltpu.VMEM((4 * c, total), F32), full(F32), full(BF16), full(F32), full(BF16), full(F32),
@@ -341,7 +379,9 @@
         pltpu.VMEM((c, 1), F32), pltpu.VMEM((c, 1), F32),
         pltpu.VMEM((n, per, wide), BF16), pltpu.VMEM((n, per, wide), BF16),
         pltpu.VMEM((per, wide), BF16), pltpu.VMEM((n, per, wide), BF16),
-        pltpu.SemaphoreType.DMA((11, n)), pltpu.SemaphoreType.DMA((11, n)),
+        pltpu.VMEM((n, per, 2 * c), BF16), pltpu.VMEM((n, per, 2 * c), BF16),
+        pltpu.VMEM((per, 2 * c), BF16), pltpu.VMEM((n, per, 2 * c), BF16),
+        pltpu.SemaphoreType.DMA((13 * (total // lc),)), pltpu.SemaphoreType.DMA((13 * (total // lc),)),
     ]
     vmem = pl.BlockSpec(memory_space=pltpu.VMEM)
     grad, gp, gg, gf, gains = pl.pallas_call(

time: 105 us -> 94.5 us (0.900)
  Pallas kernels: 95.4 us -> 84.5 us
    pallas_call x1, Pallas kernels: 95.4 us -> 84.5 us  [shards(): pl.pallas_call(functools.partial(kernel, n, rows, res, lc), out_shape=(ja...]
where the time goes in v2:
time: 94.5 us; the launch traced here: 94.2 us
  Pallas kernels  84.5 us (89%)
  local copies, waits for them, and re-layouts  8.22 us (9%)
    pallas_call x1, Pallas kernels, shards(): pl.pallas_call(functools.partial(kernel, n, rows, res, lc), out_shape=(ja...  84.5 us
    unnamed x24, local copies, waits for them, and re-layouts  6.02 us

profile of v2, /device:TPU:0, one launch (start us, length us, event | category | flops | bytes accessed | tf_op | source)
XLA Modules:
  0.0 94.2 jit_solution(18424968762924644302)
XLA Ops:
  0.6 0.6 copy-done.4
  1.3 0.1 dynamic_slice.6
  1.4 0.1 multiply_convert_fusion
  1.4 0.1 convert_element_type.27
  1.5 0.6 copy-done.5
  2.1 0.1 dynamic_slice.7
  2.2 0.1 compare_convert_fusion
  2.2 0.1 reshape.81
  2.3 0.6 pad_maximum_fusion.masks
  3.0 0.0 copy-start.6
  3.0 0.6 copy-done.7
  3.6 0.0 copy-done.8
  3.6 0.0 copy-done.9
  3.6 0.0 copy-done.3
  3.7 0.0 copy-done.6
  3.7 0.6 concatenate.3.params
  4.3 84.5 %shard_map.190 = (bf16[1152,128]{1,0:T(8,128)(2,1)}, f32[128,512]{1,0:T(8,128)}, f32[128,128]{1,0:T(8,128)}, f32[128,128]{1,0:T(8,128)}, f32[8,128]{1,0:T(8,128)}) custom-call(bf16[1152,128]{1,0:T(8,128)(2,1)} %bitcast.11, bf16[1152,128]{1,0:T(8,128)(2,1)} %bitcast.12, f32[2,1152]{1,0:T(2,128)} %pad_maximum_fusion.masks, f32[8,128]{1,0:T(8,128)} %concatenate.3.params, ...), custom_call_target="tpu_custom_call" | custom-call | tf_op jit(solution)/shard_map/pallas_call | solution.py:387
  88.8 1.3 %slice_bitcast_fusion = (f32[128]{0:T(128)}, f32[128]{0:T(128)}) fusion(f32[8,128]{1,0:T(8,128)} %get-tuple-element.15), kind=kLoop, calls=%fused_computation.3 | loop fusion | bytes 2048 | tf_op jit(solution)/shard_map/squeeze | solution.py:406
  90.1 1.7 %copy.25 = bf16[12,96,128]{2,1,0:T(8,128)(2,1)} copy(bf16[12,96,128]{2,1,0:T(8,128)(2,1)} %bitcast.13) | data formatting | bytes 589824
  91.9 0.7 copy.26
  92.6 0.2 copy-done.2
  92.7 0.6 copy.27
  93.4 0.2 copy-done.1
  93.6 0.6 copy.28
  (11 shorter events, 0.0 us)
Async XLA Ops:
  0.6 0.7 copy-start.4
  1.4 0.7 copy-start.5
  2.9 0.7 copy-start.7
  2.9 0.7 copy-start.8
  3.0 0.7 copy-start.9
  3.0 0.7 copy-start.3
  3.0 0.7 copy-start.6
  90.1 1.7 %copy-start = (f32[128,512]{1,0:T(8,128)S(1)}, f32[128,512]{1,0:T(8,128)}, u32[]{:S(2)}) copy-start(f32[128,512]{1,0:T(8,128)} %get-tuple-element.25) | copy-start | bytes 786436
  91.9 0.9 copy-start.2
  92.7 0.9 copy-start.1

commit v3 on v2

--- a/solution.py
+++ b/solution.py
@@ -10,7 +10,7 @@
 F32 = jnp.float32
 BF16 = jnp.bfloat16
 LANES = 128
-A_OUT, B_OUT, X_OUT, A_IN, B_IN, X_IN, G_X, G_A, G_B, P_SUM, P_ALL, H_SUM, H_ALL = range(13)
+A_OUT, B_OUT, X_OUT, A_IN, B_IN, X_IN, G_X, G_A, G_B, P_SUM, P_ALL, H_SUM, H_ALL, GAINS = range(14)
 
 
 def tn(w, x):
@@ -48,14 +48,14 @@
 
 def kernel(
     n, rows, res, lc,
-    pair, cot, masks, params, out_proj, out_gate, out_final, in_proj, in_gate, in_final,
-    grad_out, gp_out, gg_out, gf_out, gains_out,
-    cols, start, normed, gate, in_p, cot_t, mid, logit_s, gv, gy, gl,
+    pair, cot, residues, chains, embed, gain_on, gain_om, gain_in, gain_im, out_proj, out_gate, out_final, in_proj, in_gate, in_final,
+    grad_out, gp_out, gg_out, gf_out, gn_out, gm_out,
+    cols, masks, in_q, start, normed, gate, in_p, cot_t, mid, logit_s, gv, gy, gl,
     a_s, b_s, x_s, a_r, b_r, x_r,
     a2_s, b2_s, x2_s, a2_r, b2_r, x2_r,
     gx_s, gx_r, ga_s, gb_s, ga_r, gb_r,
-    slab_a, slab_b, slab_o, slab_p, mat_a, mat_b,
-    acc_p, acc_g, acc_f, acc_n, acc_m, g_s, g_r, t_s, t_r, h_s, h_r, u_s, u_r,
+    slab_a, slab_b, slab_o, slab_p, mat_a, mat_b, mat_x,
+    acc_p, acc_g, acc_f, acc_n, acc_m, g_s, g_r, t_s, t_r, h_s, h_r, u_s, u_r, w_s, w_r,
     send_sem, recv_sem,
 ):
     me = lax.axis_index("dap")
@@ -73,7 +73,6 @@
             barrier, inc=1, device_id={"dap": lax.rem(me + p, n)},
             device_id_type=pl.DeviceIdType.MESH,
         )
-    pl.semaphore_wait(barrier, n - 1)
 
     def copy_to(sem, src, dst, peer):
         return pltpu.make_async_remote_copy(
@@ -160,12 +159,21 @@
         copy_to(which * chunks, block, block, lax.rem(me + 1, n)).wait()
         return dst[...].astype(F32).reshape(c, dst.shape[2])
 
-    cols[...] = params[...].T
+    params = [embed[...], gain_on[...], gain_om[...], gain_in[...], gain_im[...]]
+    cols[...] = jnp.concatenate(params + [jnp.zeros((2, c), F32)], axis=0).T
+    here = lax.broadcasted_iota(jnp.int32, (rows, res), 1) == (
+        lax.broadcasted_iota(jnp.int32, (rows, res), 0) + me * rows
+    )
+    row_mask = jnp.sum(jnp.where(here, residues[...], 0).astype(F32), axis=1, keepdims=True)
+    row_chain = jnp.sum(jnp.where(here, chains[...], 0).astype(F32), axis=1, keepdims=True)
+    both = row_mask * residues[...].astype(F32)
+    same_chain = jnp.where(row_chain == chains[...].astype(F32), 1.0, 0.0)
+    masks[0:1, :] = jnp.concatenate([both[i : i + 1] for i in range(rows)], axis=1)
+    masks[1:2, :] = jnp.concatenate([same_chain[i : i + 1] for i in range(rows)], axis=1)
     emb0, emb1 = cols[:, 0:1], cols[:, 1:2]
     g_on, g_om, g_in, g_im = (cols[:, q : q + 1] for q in range(2, 6))
 
-    @pl.loop(0, chunks)
-    def _(k):
+    def project(k):
         ds = lanes_of(k)
         same = masks[1:2, ds] > 0.5
         x = pair[ds, :].astype(F32).T + jnp.where(same, emb1, emb0)
@@ -177,7 +185,15 @@
         pm = masks[0:1, ds]
         put(a_s, ds, pm * sigmoid(p[:c]) * p[c : 2 * c])
         put(b_s, ds, pm * sigmoid(p[2 * c : 3 * c]) * p[3 * c :])
-        spread(B_OUT, b_s, b_r, k, ds)
+
+    project(0)
+    pl.semaphore_wait(barrier, n - 1)
+    spread(B_OUT, b_s, b_r, 0, lanes_of(0))
+
+    @pl.loop(1, chunks)
+    def _(k):
+        project(k)
+        spread(B_OUT, b_s, b_r, k, lanes_of(k))
 
     @pl.loop(0, chunks)
     def _(k):
@@ -295,13 +311,19 @@
 
     for ch in range(per):
         gx = matrix(slab_a, ch)
+        mat_x[ch] = gx
         keep(slab_o, ch, nt(mat_b[ch], gx))
-        keep(slab_p, ch, nn(mat_a[ch], gx))
 
     @pl.loop(0, chunks)
     def _(k):
         from_slab(slab_o, ga_s, k)
         spread(G_A, ga_s, ga_r, k, lanes_of(k))
+
+    for ch in range(per):
+        keep(slab_p, ch, nn(mat_a[ch], mat_x[ch]))
+
+    @pl.loop(0, chunks)
+    def _(k):
         from_slab(slab_p, gb_s, k)
         spread(G_B, gb_s, gb_r, k, lanes_of(k))
 
@@ -321,8 +343,16 @@
         q0 = (ga * in_p[c : 2 * c, ds] * (1.0 - s0)).astype(BF16)
         q2 = (gb * in_p[3 * c :, ds] * (1.0 - s2)).astype(BF16)
         q = jnp.concatenate([q0, ga.astype(BF16), q2, gb.astype(BF16)], axis=0)
+        in_q[:, ds] = q
         acc_p[...] += nt(normed[:, ds], q)
-        g = nn(in_proj[...], q) + gy[:, ds]
+
+    g_s[...] = (acc_p[...] * inv_count).reshape(n, per, 4 * c).astype(BF16)
+    spread(P_SUM, g_s, g_r)
+
+    @pl.loop(0, chunks)
+    def _(k):
+        ds = lanes_of(k)
+        g = nn(in_proj[...], in_q[:, ds]) + gy[:, ds]
         hat, inv = norm_stats(mid[:, ds].astype(F32))
         acc_n[...] += lane_sum(g * hat)
         z = cot_t[:, ds] + norm_back(g, hat, inv, g_in)
@@ -330,17 +360,21 @@
 
     lane = lax.broadcasted_iota(jnp.int32, (c, LANES), 1)
     gains = jnp.where(lane == 0, acc_n[...], jnp.where(lane == 1, acc_m[...], 0.0))
-    whole = jnp.concatenate([acc_p[...], gains], axis=1) * inv_count
-    g_s[...] = whole.reshape(n, per, whole.shape[1]).astype(BF16)
-    spread(P_SUM, g_s, g_r)
+    w_s[...] = (gains * inv_count).T[:8]
+    for p in range(1, n):
+        copy_to(GAINS * chunks, w_s, w_r.at[me], lax.rem(me + p, n)).start()
+    w_r[me] = w_s[...]
+    collect(P_SUM, g_s, g_r)
+    hand_round(P_ALL, g_r, t_s, t_r)
     both = gathered(H_ALL, u_r)
     gg_out[...] = both[:, :c]
     gf_out[...] = both[:, c:]
-    collect(P_SUM, g_s, g_r)
-    hand_round(P_ALL, g_r, t_s, t_r)
-    final = gathered(P_ALL, t_r)
-    gp_out[...] = final[:, : 4 * c]
-    gains_out[...] = final[:, 4 * c :].T[:8]
+    block = w_r.at[pl.ds(0, n - 1)]
+    copy_to(GAINS * chunks, block, block, lax.rem(me + 1, n)).wait()
+    gain_sums = jnp.sum(w_r[...], axis=0)
+    gn_out[...] = gain_sums[0:1]
+    gm_out[...] = gain_sums[1:2]
+    gp_out[...] = gathered(P_ALL, t_r)
 
 
 def shards(n, pair, cotangent, residue_mask, chain_ids, chain_embed, out_norm_gain, out_proj,
@@ -353,57 +387,52 @@
         if rows % q == 0 and q * res % LANES == 0 and (rows // q <= 3)
     )
     tiles = -(-res // LANES)
-    row_start = lax.axis_index("dap") * rows
-    row_mask = lax.dynamic_slice_in_dim(residue_mask, row_start, rows, 0)
-    row_chain = lax.dynamic_slice_in_dim(chain_ids, row_start, rows, 0)
-    pair_mask = (row_mask[:, None] * residue_mask[None, :]).astype(F32)
-    same = (row_chain[:, None] == chain_ids[None, :]).astype(F32)
-    masks = jnp.stack([pair_mask.reshape(total), same.reshape(total)])
-    params = jnp.concatenate(
-        [chain_embed, jnp.stack([out_norm_gain, out_mid_gain, in_norm_gain, in_mid_gain]),
-         jnp.zeros((2, c), F32)], axis=0)
-
     def full(dtype):
         return pltpu.VMEM((c, total), dtype)
 
     swap = pltpu.VMEM((n, per, total), BF16)
     slab = pltpu.VMEM((tiles, res * per, LANES), F32)
     mats = pltpu.VMEM((per, res, res), BF16)
-    wide = 4 * c + LANES
+    wide = 4 * c
     scratch = [
-        pltpu.VMEM((c, 8), F32), full(F32), full(BF16), full(F32),
+        pltpu.VMEM((c, 8), F32), pltpu.VMEM((2, total), F32), pltpu.VMEM((4 * c, total), BF16), full(F32), full(BF16), full(F32),
         pltpu.VMEM((4 * c, total), F32), full(F32), full(BF16), full(F32), full(BF16), full(F32),
         full(BF16),
-    ] + [swap] * 18 + [slab] * 4 + [mats] * 2 + [
+    ] + [swap] * 18 + [slab] * 4 + [mats] * 3 + [
         pltpu.VMEM((c, 4 * c), F32), pltpu.VMEM((c, c), F32), pltpu.VMEM((c, c), F32),
         pltpu.VMEM((c, 1), F32), pltpu.VMEM((c, 1), F32),
         pltpu.VMEM((n, per, wide), BF16), pltpu.VMEM((n, per, wide), BF16),
         pltpu.VMEM((per, wide), BF16), pltpu.VMEM((n, per, wide), BF16),
         pltpu.VMEM((n, per, 2 * c), BF16), pltpu.VMEM((n, per, 2 * c), BF16),
         pltpu.VMEM((per, 2 * c), BF16), pltpu.VMEM((n, per, 2 * c), BF16),
-        pltpu.SemaphoreType.DMA((13 * (total // lc),)), pltpu.SemaphoreType.DMA((13 * (total // lc),)),
+        pltpu.VMEM((8, c), F32), pltpu.VMEM((n, 8, c), F32),
+        pltpu.SemaphoreType.DMA((14 * (total // lc),)), pltpu.SemaphoreType.DMA((14 * (total // lc),)),
     ]
     vmem = pl.BlockSpec(memory_space=pltpu.VMEM)
-    grad, gp, gg, gf, gains = pl.pallas_call(
+    grad, gp, gg, gf, gn, gm = pl.pallas_call(
         functools.partial(kernel, n, rows, res, lc),
         out_shape=(
             jax.ShapeDtypeStruct((total, c), BF16),
             jax.ShapeDtypeStruct((c, 4 * c), F32),
             jax.ShapeDtypeStruct((c, c), F32),
             jax.ShapeDtypeStruct((c, c), F32),
-            jax.ShapeDtypeStruct((8, c), F32),
+            jax.ShapeDtypeStruct((1, c), F32),
+            jax.ShapeDtypeStruct((1, c), F32),
         ),
-        in_specs=[vmem] * 10,
-        out_specs=(vmem,) * 5,
+        in_specs=[vmem] * 15,
+        out_specs=(vmem,) * 6,
         scratch_shapes=scratch,
         compiler_params=pltpu.CompilerParams(
             collective_id=0, has_side_effects=True, vmem_limit_bytes=60 * 1024 * 1024
         ),
     )(
-        pair.reshape(total, c), cotangent.reshape(total, c), masks, params,
+        pair.reshape(total, c), cotangent.reshape(total, c),
+        residue_mask.reshape(1, res), chain_ids.reshape(1, res), chain_embed,
+        out_norm_gain.reshape(1, c), out_mid_gain.reshape(1, c),
+        in_norm_gain.reshape(1, c), in_mid_gain.reshape(1, c),
         out_proj, out_gate, out_final, in_proj, in_gate, in_final,
     )
-    return grad.reshape(rows, res, c), gp, gg, gf, gains[0], gains[1]
+    return grad.reshape(rows, res, c), gp, gg, gf, gn.reshape(c), gm.reshape(c)
 
 
 def solution(mesh):

time: 94.5 us -> 88.7 us (0.939)
  local copies, waits for them, and re-layouts: 8.22 us -> 5.21 us
  Pallas kernels: 84.5 us -> 82.5 us
    pallas_call x1, Pallas kernels: 84.5 us -> 82.5 us  [shards(): pl.pallas_call(functools.partial(kernel, n, rows, res, lc), out_shape=(ja...]
    squeeze x1 -> x0, local copies, waits for them, and re-layouts: 1.28 us -> none  [shards(): return (grad.reshape(rows, res, c), gp, gg, gf, gains[0], gains[1])]
    unnamed x24 -> x16, local copies, waits for them, and re-layouts: 6.02 us -> 5.21 us
where the time goes in v3:
time: 88.7 us; the launch traced here: 88.4 us
  Pallas kernels  82.5 us (93%)
  local copies, waits for them, and re-layouts  5.21 us (6%)
    pallas_call x1, Pallas kernels, shards(): pl.pallas_call(functools.partial(kernel, n, rows, res, lc), out_shape=(ja...  82.5 us
    unnamed x16, local copies, waits for them, and re-layouts  5.21 us

profile of v3, /device:TPU:0, one launch (start us, length us, event | category | flops | bytes accessed | tf_op | source)
XLA Modules:
  0.0 88.4 jit_solution(5351483375776239998)
XLA Ops:
  0.6 82.5 %shard_map.190 = (bf16[1152,128]{1,0:T(8,128)(2,1)}, f32[128,512]{1,0:T(8,128)}, f32[128,128]{1,0:T(8,128)}, f32[128,128]{1,0:T(8,128)}, f32[1,128]{1,0:T(1,128)}, /*index=5*/f32[1,128]{1,0:T(1,128)}) custom-call(bf16[1152,128]{1,0:T(8,128)(2,1)} %bitcast.12, bf16[1152,128]{1,0:T(8,128)(2,1)} %bitcast.13, s32[1,96]{1,0:T(1,128)} %bitcast.14, ...), custom_call_target="tpu_custom_call" | custom-call | tf_op jit(solution)/shard_map/pallas_call | solution.py:412
  83.2 0.0 copy-start
  83.2 1.7 %copy.27 = bf16[12,96,128]{2,1,0:T(8,128)(2,1)} copy(bf16[12,96,128]{2,1,0:T(8,128)(2,1)} %bitcast.11) | data formatting | bytes 589824
  84.9 0.0 copy-done
  84.9 0.0 copy-start.2
  84.9 0.7 copy.28
  85.6 0.2 copy-done.2
  85.8 0.0 copy-start.1
  85.8 0.6 copy.29
  86.4 0.2 copy-done.1
  86.7 0.0 copy-start.4
  86.7 0.6 copy.30
  87.3 0.0 copy-done.4
  87.3 0.0 copy-start.3
  87.3 0.5 copy.31
  87.8 0.1 copy-done.3
  87.9 0.5 copy.32
Async XLA Ops:
  83.2 1.7 %copy-start = (f32[128,512]{1,0:T(8,128)S(1)}, f32[128,512]{1,0:T(8,128)}, u32[]{:S(2)}) copy-start(f32[128,512]{1,0:T(8,128)} %get-tuple-element.25) | copy-start | bytes 786436
  84.9 0.9 copy-start.2
  85.8 0.9 copy-start.1
  86.7 0.7 copy-start.4
  87.3 0.6 copy-start.3
